TPU v7x, 32 devices: a whole 2x2x4 slice. The times are simulated.
32 devices in a mesh: dp: 8 (over z, y), expert: 4 (over x, core).
Axes of the slice: x: 2, y: 2, z: 4, core: 2. Of those that a mesh axis runs over, the one named last changes fastest.
Arguments:
- queries: bfloat16 [4096, 4096], P('dp', 'expert'), may hold values from -6 to 6
- key_states: bfloat16 [4096, 4096], P('dp', 'expert'), may hold values from -6 to 6
- value_states: bfloat16 [4096, 4096], P('dp', 'expert'), may hold values from -6 to 6
- doc_lengths: int32 [8, 8], replicated, may hold values from 0 to 512, as said below
- move_plan: int32 [8, 2], replicated, may hold values from 0 to 7, as said below
- expert_ids: int32 [4096, 8], P('dp'), may hold values from 0 to 15, all different within a row; in each aligned block of 512 rows (0 to 511, 512 to 1023, ...) at most 384 rows name the same one
- gate_weights: float32 [4096, 8], P('dp'), may hold values from 0.05 to 0.5
- expert_weight: bfloat16 [16, 4096, 1024], P('expert'), may hold values from -0.29882812 to 0.29882812
Outputs:
- attended: bfloat16 [4096, 4096], P('dp', 'expert')
- combined: bfloat16 [4096, 1024], P('dp', 'expert')
- row_load: float32 [8], P('dp')
Inputs may be any that keep to these rules, and one draw needn't show every extreme that they name: `doc_lengths`: each row's entries are the lengths of its packed documents in order and sum to 512; a zero marks an absent document; some row holds a single document. move_plan[r, 0] is r itself or the row half the dp axis away, (r + 8 / 2) mod 8; a row is handed to its partner only if its pairs in all exceed the partner's, so two partners never both move; move_plan[r, 1] is a block number below 2; at least one row moves a block. `expert_ids`: each token names 8 different experts; among the 512 tokens of one row no expert is named by more than 384 tokens.
All inputs are finite; a program needn't handle non-finite values.
Results may differ from a plain program's by a relative error of at most 0.0095.
Values may be sent and summed in bfloat16 or wider, within the bound.
A program may use at most 128 MiB of HBM per device.

v0:
```python
import functools

import jax
import jax.numpy as jnp
from jax import lax
from jax.experimental import pallas as pl
from jax.experimental.pallas import tpu as pltpu
from jax.sharding import PartitionSpec as P

HEAD_DIM = 128
QBLOCK = 128
MESH = pl.DeviceIdType.MESH
LOG2E = 1.4426950408889634


def span_pairs(low, high, start, stop):
    first = jnp.maximum(low, start)
    last = jnp.minimum(high, stop)
    count = jnp.maximum(last - first, 0)
    return (count * ((first - start + 1) + (last - start))) // 2


def row_pairs(lens, row, block, docs, row_count):
    low = block * QBLOCK
    total = jnp.int32(0)
    picked = jnp.int32(0)
    edge = jnp.int32(0)
    for doc in range(docs):
        stop = edge + lens[row, doc]
        total = total + span_pairs(0, row_count, edge, stop)
        picked = picked + span_pairs(low, low + QBLOCK, edge, stop)
        edge = stop
    return total, picked


def kernel(dp_size, group, q_hbm, k_hbm, v_hbm, lens, plan, ids, gates, w_hbm,
           att_hbm, comb, load,
           qv, kv, vv, wv, xg, acc, bias, gsc, part, rxd, txx, rxx,
           in_sem, w_sem, out_sem,
           sx_sem, rx_sem, sd_sem, rd_sem, sf_sem, rf_sem,
           ps_sem, pr_sem, qs_sem, qr_sem):
    rows, width = q_hbm.shape
    experts, depth, ff = w_hbm.shape
    chips = group // 2
    ck = qv.shape[1] // att_chunks(width)
    chunks = width // ck
    chip_width = 2 * width
    step_width = 2 * ck
    owned = ff // group
    row = lax.axis_index("dp")
    me = lax.axis_index("expert")
    chip = me // 2
    core = lax.rem(me, 2)
    other = chip * 2 + 1 - core

    def in_copies(c):
        cols = pl.ds(pl.multiple_of(c * ck, 128), ck)
        return [
            pltpu.make_async_copy(src.at[:, cols], dst.at[:, cols], in_sem.at[i, c])
            for i, (src, dst) in enumerate(((q_hbm, qv), (k_hbm, kv), (v_hbm, vv)))
        ]

    def place(s, c, k):
        return pl.multiple_of(s * chip_width + c * step_width + k * ck, 128)

    def w_copy(e, s, c, k):
        src = pl.multiple_of((s * 2 + k) * width + c * ck, 128)
        return pltpu.make_async_copy(
            w_hbm.at[e, pl.ds(src, ck), :], wv.at[e, pl.ds(place(s, c, k), ck), :],
            w_sem.at[e, s, c, k])

    def w_start(e, s, c):
        for k in range(2):
            w_copy(e, s, c, k).start()

    def w_wait(e, s, c):
        for k in range(2):
            w_copy(e, s, c, k).wait()

    for c in range(chunks):
        for copy in in_copies(c):
            copy.start()

    barrier = pltpu.get_barrier_semaphore()
    pl.semaphore_signal(barrier, inc=1, device_id={"expert": other}, device_id_type=MESH)
    for d in range(1, chips):
        peer = lax.rem(chip + d, chips) * 2 + core
        pl.semaphore_signal(barrier, inc=1, device_id={"expert": peer}, device_id_type=MESH)

    def start_own(i, _):
        w_start(i // chunks, chip, lax.rem(i, chunks))
        return 0

    lax.fori_loop(0, experts * chunks, start_own, 0)
    docs = lens.shape[1]
    pos = lax.broadcasted_iota(jnp.int32, (rows, rows), 0)
    key_pos = lax.broadcasted_iota(jnp.int32, (rows, rows), 1)
    column = lax.broadcasted_iota(jnp.int32, (rows, 1), 0)
    starts = jnp.zeros((rows, 1), jnp.int32)
    edge = jnp.int32(0)
    for doc in range(docs):
        edge = edge + lens[row, doc]
        starts = jnp.where(column >= edge, jnp.maximum(starts, edge), starts)
    bias[...] = jnp.where((key_pos <= pos) & (key_pos >= starts), 0.0, -1e30)

    pl.semaphore_wait(barrier, chips)

    half = rows // 2

    def band_of(b):
        return pl.ds(b * half, half)

    def cross_copy(b, c, d):
        at = xg.at[band_of(b), pl.ds(place(chip, c, core), ck)]
        return pltpu.make_async_remote_copy(
            src_ref=at, dst_ref=at,
            send_sem=sx_sem.at[d - 1, b, c], recv_sem=rx_sem.at[d - 1, b, c],
            device_id={"expert": lax.rem(chip + d, chips) * 2 + core}, device_id_type=MESH)

    def side_copy(b, c):
        at = xg.at[band_of(b), pl.ds(place(chip, c, core), ck)]
        return pltpu.make_async_remote_copy(
            src_ref=at, dst_ref=at,
            send_sem=sd_sem.at[b, c], recv_sem=rd_sem.at[b, c],
            device_id={"expert": other}, device_id_type=MESH)

    def pass_copy(b, c, d):
        at = xg.at[band_of(b), pl.ds(place(lax.rem(chip - d + chips, chips), c, core), ck)]
        return pltpu.make_async_remote_copy(
            src_ref=at, dst_ref=at,
            send_sem=sf_sem.at[d - 1, b, c], recv_sem=rf_sem.at[d - 1, b, c],
            device_id={"expert": other}, device_id_type=MESH)

    def out_copy(c):
        return pltpu.make_async_copy(
            xg.at[:, pl.ds(place(chip, c, core), ck)],
            att_hbm.at[:, pl.ds(pl.multiple_of(c * ck, 128), ck)], out_sem.at[c])

    scale = HEAD_DIM ** -0.5 * LOG2E

    for b in range(2):
        low, high = b * half, (b + 1) * half

        def attend(c, _, b=b, low=low, high=high):
            if b == 0:
                for copy in in_copies(c):
                    copy.wait()
            for h in range(ck // HEAD_DIM):
                cols = pl.ds(pl.multiple_of(c * ck + h * HEAD_DIM, 128), HEAD_DIM)
                dst = pl.ds(pl.multiple_of(place(chip, c, core) + h * HEAD_DIM, 128), HEAD_DIM)
                s = lax.dot_general(
                    qv[low:high, cols], kv[:high, cols], (((1,), (1,)), ((), ())),
                    preferred_element_type=jnp.float32)
                s = s + bias[low:high, :high]
                top = jnp.max(s, axis=1, keepdims=True)
                p = jnp.exp2((s - top) * scale)
                norm = jnp.sum(p, axis=1, keepdims=True)
                o = jnp.dot(p.astype(jnp.bfloat16), vv[:high, cols],
                            preferred_element_type=jnp.float32)
                xg[low:high, dst] = (o / norm).astype(jnp.bfloat16)
            for d in range(1, chips):
                cross_copy(b, c, d).start()
            side_copy(b, c).start()
            if b == 1:
                out_copy(c).start()
            return 0

        lax.fori_loop(0, chunks, attend, 0)

    for d in range(1, chips):
        def start_far(i, _, d=d):
            w_start(lax.rem(i, experts), lax.rem(chip - d + chips, chips), i // experts)
            return 0

        lax.fori_loop(0, experts * chunks, start_far, 0)

    partner = lax.rem(row + dp_size // 2, dp_size)
    own_total, own_moved = row_pairs(lens, row, plan[1, row], docs, rows)
    _, their_moved = row_pairs(lens, partner, plan[1, partner], docs, rows)
    work = own_total - jnp.where(plan[0, row] != row, own_moved, 0)
    work = work + jnp.where(plan[0, partner] != partner, their_moved, 0)
    load[0] = work.astype(jnp.float32) * (1.0 / (QBLOCK * QBLOCK))

    for e in range(experts):
        chosen = ids[...] == me * experts + e
        line = jnp.sum(jnp.where(chosen, gates[...], 0.0), axis=0, keepdims=True)
        for r in range(0, rows, 128):
            gsc[e, r:r + 128, :] = jnp.broadcast_to(line[:, r:r + 128], (128, 128)).T

    forwards = [(b, c, d) for b in range(2) for c in range(chunks) for d in range(1, chips)]
    per_half = len(forwards) // 2
    sent = [0]

    def forward(count):
        while sent[0] < min(count, len(forwards)):
            b, c, d = forwards[sent[0]]
            cross_copy(b, c, d).wait_recv()
            pass_copy(b, c, d).start()
            sent[0] += 1

    forward(1)
    for b in range(2):
        for c in range(chunks):
            side_copy(b, c).wait_recv()
    own = pl.ds(pl.multiple_of(chip * chip_width, 128), chip_width)
    tile = ff // 2
    for e in range(experts):
        def wait_own(c, _, e=e):
            w_wait(e, chip, c)
            return 0

        lax.fori_loop(0, chunks, wait_own, 0)

        def near(t, _, e=e):
            cols = pl.ds(pl.multiple_of(t * tile, 128), tile)
            acc[e, :, cols] = jnp.dot(xg[:, own], wv[e, own, cols],
                                      preferred_element_type=jnp.float32)
            return 0

        lax.fori_loop(0, 2, near, 0)
        forward(min(sent[0] + 1, per_half))

    def pair_copy(b, j):
        return pltpu.make_async_remote_copy(
            src_ref=part.at[j * 2 + 1 - core, band_of(b)], dst_ref=rxd.at[j, band_of(b)],
            send_sem=ps_sem.at[b, j], recv_sem=pr_sem.at[b, j],
            device_id={"expert": other}, device_id_type=MESH)

    def sum_copy(b, d):
        return pltpu.make_async_remote_copy(
            src_ref=txx.at[d - 1, band_of(b)], dst_ref=rxx.at[d - 1, band_of(b)],
            send_sem=qs_sem.at[b, d - 1], recv_sem=qr_sem.at[b, d - 1],
            device_id={"expert": lax.rem(chip + d, chips) * 2 + core}, device_id_type=MESH)

    def exchange(b):
        at = band_of(b)
        for d in range(1, chips):
            j = lax.rem(chip + d, chips)
            pair_copy(b, j).wait_recv()
            txx[d - 1, at, :] = (part[j * 2 + core, at, :].astype(jnp.float32)
                                 + rxd[j, at, :].astype(jnp.float32)).astype(jnp.bfloat16)
            sum_copy(b, d).start()

    def arrive(b, c0, c1, d):
        for c in range(c0, c1):
            forward(forwards.index((b, c, d)) + 1)
        for c in range(c0, c1):
            pass_copy(b, c, d).wait_recv()
            if b == 0:
                def wait_far(e, _, c=c, d=d):
                    w_wait(e, lax.rem(chip - d + chips, chips), c)
                    return 0

                lax.fori_loop(0, experts, wait_far, 0)
        return pl.ds(place(lax.rem(chip - d + chips, chips), c0, 0), (c1 - c0) * step_width)

    columns = 2 * owned
    rt = 64

    def add_far(b, e, span, cols):
        at = band_of(b)
        acc[e, at, cols] += jnp.dot(xg[at, span], wv[e, span, cols],
                                    preferred_element_type=jnp.float32)

    def close(b, span):
        for d in list(range(1, chips)) + [0]:
            j = lax.rem(chip + d, chips)
            cols = pl.ds(pl.multiple_of(j * columns, 128), columns)
            for e in range(experts):
                add_far(b, e, span, cols)

            def finish(r, _, cols=cols, j=j):
                at = pl.ds(pl.multiple_of(b * half + r * rt, rt), rt)
                total = jnp.zeros((rt, columns), jnp.float32)
                for e in range(experts):
                    h = acc[e, at, cols] * 0.5
                    total = total + (h * jnp.tanh(h) + h) * jnp.concatenate(
                        [gsc[e, at, :]] * (columns // 128), axis=1)
                total = total.astype(jnp.bfloat16)
                part[j * 2, at, :] = total[:, :owned]
                part[j * 2 + 1, at, :] = total[:, owned:]
                return 0

            lax.fori_loop(0, half // rt, finish, 0)
            pair_copy(b, j).start()

    whole = pl.ds(0, ff)
    for d in range(1, chips):
        span = arrive(0, 0, chunks, d)
        if d < chips - 1:
            for e in range(experts):
                add_far(0, e, span, whole)
    forward(per_half + 1)
    close(0, span)
    forward(per_half + 2)
    exchanged = False
    if chunks > 1:
        for d in range(1, chips):
            span = arrive(1, 0, chunks - 1, d)
            for e in range(experts):
                add_far(1, e, span, whole)
                if e == 0 and not exchanged:
                    exchange(0)
                    exchanged = True
                if d == chips - 1 and e == experts // 2:
                    forward(len(forwards))
    if not exchanged:
        exchange(0)
    for d in range(1, chips):
        span = arrive(1, chunks - 1, chunks, d)
        if d < chips - 1:
            for e in range(experts):
                add_far(1, e, span, whole)
    close(1, span)
    exchange(1)
    for b in range(2):
        at = band_of(b)
        pair_copy(b, chip).wait_recv()
        total = (part[chip * 2 + core, at, :].astype(jnp.float32)
                 + rxd[chip, at, :].astype(jnp.float32))
        for d in range(1, chips):
            sum_copy(b, d).wait_recv()
            total = total + rxx[d - 1, at, :].astype(jnp.float32)
        comb[at, :] = total.astype(jnp.bfloat16)

    for c in range(chunks):
        out_copy(c).wait()
        for b in range(2):
            side_copy(b, c).wait_send()
            for d in range(1, chips):
                cross_copy(b, c, d).wait_send()
                pass_copy(b, c, d).wait_send()
    for b in range(2):
        for j in range(chips):
            pair_copy(b, j).wait_send()
        for d in range(1, chips):
            sum_copy(b, d).wait_send()


def att_chunks(width):
    return width // (2 * HEAD_DIM)


def shards(dp_size, group, queries, key_states, value_states, doc_lengths, move_plan,
           expert_ids, gate_weights, expert_weight):
    rows, width = queries.shape
    experts, depth, ff = expert_weight.shape
    chips = group // 2
    chunks = att_chunks(width)
    owned = ff // group
    bf16, f32 = jnp.bfloat16, jnp.float32
    hbm = pl.BlockSpec(memory_space=pl.ANY)
    smem = pl.BlockSpec(memory_space=pltpu.SMEM)
    vmem = pl.BlockSpec(memory_space=pltpu.VMEM)
    dma = pltpu.SemaphoreType.DMA
    return pl.pallas_call(
        functools.partial(kernel, dp_size, group),
        out_shape=(
            jax.ShapeDtypeStruct((rows, width), bf16),
            jax.ShapeDtypeStruct((rows, owned), bf16),
            jax.ShapeDtypeStruct((1,), f32),
        ),
        in_specs=[hbm, hbm, hbm, smem, smem, vmem, vmem, hbm],
        out_specs=(hbm, vmem, smem),
        scratch_shapes=[
            pltpu.VMEM((rows, width), bf16),
            pltpu.VMEM((rows, width), bf16),
            pltpu.VMEM((rows, width), bf16),
            pltpu.VMEM((experts, depth, ff), bf16),
            pltpu.VMEM((rows, depth), bf16),
            pltpu.VMEM((experts, rows, ff), f32),
            pltpu.VMEM((rows, rows), f32),
            pltpu.VMEM((experts, rows, 128), f32),
            pltpu.VMEM((group, rows, owned), bf16),
            pltpu.VMEM((chips, rows, owned), bf16),
            pltpu.VMEM((chips - 1, rows, owned), bf16),
            pltpu.VMEM((chips - 1, rows, owned), bf16),
            dma((3, chunks)),
            dma((experts, chips, chunks, 2)),
            dma((chunks,)),
            dma((chips - 1, 2, chunks)),
            dma((chips - 1, 2, chunks)),
            dma((2, chunks)),
            dma((2, chunks)),
            dma((chips - 1, 2, chunks)),
            dma((chips - 1, 2, chunks)),
            dma((2, chips)),
            dma((2, chips)),
            dma((2, chips - 1)),
            dma((2, chips - 1)),
        ],
        compiler_params=pltpu.CompilerParams(
            collective_id=0, has_side_effects=True, vmem_limit_bytes=66_000_000),
    )(queries, key_states, value_states, doc_lengths, move_plan.T, expert_ids.T,
      gate_weights.T, expert_weight)


def solution(mesh):
    in_specs = (
        P("dp", "expert"),
        P("dp", "expert"),
        P("dp", "expert"),
        P(),
        P(),
        P("dp", None),
        P("dp", None),
        P("expert", None, None),
    )
    out_specs = (P("dp", "expert"), P("dp", "expert"), P("dp"))
    body = functools.partial(shards, mesh.shape["dp"], mesh.shape["expert"])
    return jax.shard_map(body, mesh=mesh, in_specs=in_specs, out_specs=out_specs, check_vma=False)
```

profile of v0, /device:TPU:0, one launch (start us, length us, event | category | flops | bytes accessed | tf_op | source)
XLA Modules:
  0.0 48.0 jit_solution(4665574342723903651)
XLA Ops:
  0.6 41.7 %shard_map.103 = (bf16[512,1024]{1,0:T(8,128)(2,1)}, bf16[512,256]{1,0:T(8,128)(2,1)}, f32[1]{0:T(128)}) custom-call(bf16[512,1024]{1,0:T(8,128)(2,1)} %q_hbm.1, bf16[512,1024]{1,0:T(8,128)(2,1)} %k_hbm.1, bf16[512,1024]{1,0:T(8,128)(2,1)} %v_hbm.1, s32[8,8]{1,0:T(8,128)} %lens.1, s32[2,8]{1,0:T(2,128)} %bitcast.5, s32[8,512]{1,0:T(8,128)} %bitcast.3, ...), custom_call_target="tpu_custom_call" | custom-call | tf_op jit(solution)/shard_map/pallas_call | solution.py:356
  42.3 2.3 %copy.14 = bf16[512,1024]{1,0:T(8,128)(2,1)} copy(bf16[512,1024]{1,0:T(8,128)(2,1)} %get-tuple-element.6) | data formatting | bytes 2097152
  44.6 1.7 %copy.15 = bf16[512,256]{1,0:T(8,128)(2,1)} copy(bf16[512,256]{1,0:T(8,128)(2,1)} %get-tuple-element.7) | data formatting | bytes 524288
where the time goes:
time: 48.3 us; the launch traced here: 48 us
  Pallas kernels  41.7 us (86%)
  local copies, waits for them, and re-layouts  3.93 us (8%)
  between operations  2.4 us (5%)
    pallas_call x1, Pallas kernels, shards(): pl.pallas_call(functools.partial(kernel, dp_size, group), out_shape=(jax....  41.7 us
    unnamed x2, local copies, waits for them, and re-layouts  3.93 us

commit v1 on v0

v1 whole, which is shorter than its diff:
```python
import contextlib
import functools

import jax
import jax.numpy as jnp
from jax import lax
from jax.experimental import pallas as pl
from jax.experimental.pallas import tpu as pltpu
from jax.sharding import PartitionSpec as P

HEAD_DIM = 128
QBLOCK = 128
MESH = pl.DeviceIdType.MESH
LOG2E = 1.4426950408889634
SLOTS = 4


def scope(name):
    return contextlib.nullcontext()


def halves_of(rows):
    return [(0, rows // 2), (rows // 2, rows)]


def bands_of(rows):
    return [(0, rows // 2), (rows // 2, rows * 7 // 8), (rows * 7 // 8, rows)]


def span_pairs(low, high, start, stop):
    first = jnp.maximum(low, start)
    last = jnp.minimum(high, stop)
    count = jnp.maximum(last - first, 0)
    return (count * ((first - start + 1) + (last - start))) // 2


def row_pairs(lens, row, block, docs, row_count):
    low = block * QBLOCK
    total = jnp.int32(0)
    picked = jnp.int32(0)
    edge = jnp.int32(0)
    for doc in range(docs):
        stop = edge + lens[row, doc]
        total = total + span_pairs(0, row_count, edge, stop)
        picked = picked + span_pairs(low, low + QBLOCK, edge, stop)
        edge = stop
    return total, picked


def kernel(dp_size, group, q_hbm, k_hbm, v_hbm, lens_hbm, plan_hbm, ids_hbm, gates_hbm, w_hbm,
           att, comb, load,
           lens, plan, ids, gates, qv, kv, vv, sv, pv, wv, xg, acc, bias, gsc, part, rxd, txx, rxx,
           rx_sem, rd_sem, rf_sem, pr_sem, qr_sem,
           small_sem, in_sem, w_sem, f_sem, sx_sem, sd_sem, sf_sem, ps_sem, qs_sem):
    rows, width = q_hbm.shape
    experts, depth, ff = w_hbm.shape
    f32, bf16 = jnp.float32, jnp.bfloat16
    chips = group // 2
    ck = 2 * HEAD_DIM
    chunks = width // ck
    heads = width // HEAD_DIM
    chip_width = 2 * width
    step = 2 * ck
    owned = ff // group
    columns = 2 * owned
    halves = halves_of(rows)
    bands = bands_of(rows)
    last = len(bands) - 1
    docs = lens.shape[1]
    row = lax.axis_index("dp")
    me = lax.axis_index("expert")
    chip = me // 2
    core = lax.rem(me, 2)
    other = chip * 2 + 1 - core

    def rel(d):
        return lax.rem(chip + d, chips)

    def back(d):
        return lax.rem(chip + chips - d, chips)

    def place(d, c, k):
        if d == 0:
            return k * width + c * ck
        return d * chip_width + c * step + k * ck

    def core_of(k):
        return core if k == 0 else 1 - core

    smalls = ((lens_hbm, lens), (plan_hbm, plan), (ids_hbm, ids), (gates_hbm, gates))

    def small_copy(i):
        return pltpu.make_async_copy(*smalls[i], small_sem.at[i])

    def in_copies(p, c):
        lo, hi = halves[p]
        cols = pl.ds(c * ck, ck)
        copies = [
            pltpu.make_async_copy(src.at[lo:hi, cols], dst.at[lo:hi, cols], in_sem.at[p, c, i])
            for i, (src, dst) in enumerate(((q_hbm, qv), (k_hbm, kv)))
        ]
        for i in range(2):
            h = 2 * c + i
            copies.append(pltpu.make_async_copy(
                v_hbm.at[lo:hi, pl.ds(h * HEAD_DIM, HEAD_DIM)],
                vv.at[h, lo:hi, pl.ds(0, HEAD_DIM)], in_sem.at[p, c, 2 + i]))
        return copies

    def cols_from(j):
        return pl.ds(pl.multiple_of(rel(j) * columns, 128), columns)

    def own_weight(e, k, j):
        return pltpu.make_async_copy(
            w_hbm.at[e, pl.ds(pl.multiple_of((chip * 2 + core_of(k)) * width, 128), width),
                     cols_from(j)],
            wv.at[e, pl.ds(k * width, width), pl.ds(j * columns, columns)],
            w_sem.at[e, k, j])

    def far_weight(e, d, c, k, j):
        return pltpu.make_async_copy(
            w_hbm.at[e, pl.ds(pl.multiple_of(
                (back(d) * 2 + core_of(k)) * width + c * ck, 128), ck), cols_from(j)],
            wv.at[e, pl.ds(place(d, c, k), ck), pl.ds(j * columns, columns)],
            f_sem.at[e, d - 1, c, k, j])

    quarters = [(k, j) for k in range(2) for j in range(chips)]

    def cross_copy(b, c, d):
        lo, hi = bands[b]
        return pltpu.make_async_remote_copy(
            src_ref=xg.at[lo:hi, pl.ds(place(0, c, 0), ck)],
            dst_ref=xg.at[lo:hi, pl.ds(place(d, c, 0), ck)],
            send_sem=sx_sem.at[d - 1, b, c], recv_sem=rx_sem.at[d - 1, b, c],
            device_id={"expert": rel(d) * 2 + core}, device_id_type=MESH)

    def side_copy(p, c):
        lo, hi = halves[p]
        return pltpu.make_async_remote_copy(
            src_ref=xg.at[lo:hi, pl.ds(place(0, c, 0), ck)],
            dst_ref=xg.at[lo:hi, pl.ds(place(0, c, 1), ck)],
            send_sem=sd_sem.at[p, c], recv_sem=rd_sem.at[p, c],
            device_id={"expert": other}, device_id_type=MESH)

    def pass_copy(b, c, d):
        lo, hi = bands[b]
        return pltpu.make_async_remote_copy(
            src_ref=xg.at[lo:hi, pl.ds(place(d, c, 0), ck)],
            dst_ref=xg.at[lo:hi, pl.ds(place(d, c, 1), ck)],
            send_sem=sf_sem.at[d - 1, b, c], recv_sem=rf_sem.at[d - 1, b, c],
            device_id={"expert": other}, device_id_type=MESH)

    def pair_copy(b, d):
        lo, hi = bands[b]
        return pltpu.make_async_remote_copy(
            src_ref=part.at[d * 2 + 1 - core, lo:hi], dst_ref=rxd.at[d, lo:hi],
            send_sem=ps_sem.at[b, d], recv_sem=pr_sem.at[b, d],
            device_id={"expert": other}, device_id_type=MESH)

    def sum_copy(b, d):
        lo, hi = bands[b]
        return pltpu.make_async_remote_copy(
            src_ref=txx.at[d - 1, lo:hi], dst_ref=rxx.at[d - 1, lo:hi],
            send_sem=qs_sem.at[b, d - 1], recv_sem=qr_sem.at[b, d - 1],
            device_id={"expert": rel(d) * 2 + core}, device_id_type=MESH)

    small_copy(0).start()
    for p in range(2):
        for c in range(chunks):
            for copy in in_copies(p, c):
                copy.start()
    for i in range(1, 4):
        small_copy(i).start()

    barrier = pltpu.get_barrier_semaphore()
    pl.semaphore_signal(barrier, inc=1, device_id={"expert": other}, device_id_type=MESH)
    for d in range(1, chips):
        pl.semaphore_signal(
            barrier, inc=1, device_id={"expert": rel(d) * 2 + core}, device_id_type=MESH)

    for h in range(heads):
        vv[h, :, HEAD_DIM:] = jnp.ones((rows, HEAD_DIM), bf16)

    with scope("lenswait"):
        small_copy(0).wait()

    def set_bias(p):
        lo, hi = halves[p]
        pos = lax.broadcasted_iota(jnp.int32, (hi - lo, hi), 0) + lo
        key_pos = lax.broadcasted_iota(jnp.int32, (hi - lo, hi), 1)
        column = lax.broadcasted_iota(jnp.int32, (hi - lo, 1), 0) + lo
        starts = jnp.zeros((hi - lo, 1), jnp.int32)
        edge = jnp.int32(0)
        for doc in range(docs):
            edge = edge + lens[row, doc]
            starts = jnp.where(column >= edge, jnp.maximum(starts, edge), starts)
        bias[lo:hi, :hi] = jnp.where((key_pos <= pos) & (key_pos >= starts), 0.0, -1e30)

    set_bias(0)

    scale = HEAD_DIM ** -0.5 * LOG2E
    units = [(p, h) for p in range(2) for h in range(heads)]

    def score(u):
        p, h = units[u]
        lo, hi = halves[p]
        cols = slice(h * HEAD_DIM, (h + 1) * HEAD_DIM)
        s = lax.dot_general(qv[lo:hi, cols], kv[:hi, cols], (((1,), (1,)), ((), ())),
                            preferred_element_type=f32)
        sv[u % SLOTS, :hi - lo, :hi] = s + bias[lo:hi, :hi]

    def soften(u):
        p, h = units[u]
        lo, hi = halves[p]
        s = sv[u % SLOTS, :hi - lo, :hi]
        top = jnp.max(s, axis=1, keepdims=True)
        pv[u % SLOTS, :hi - lo, :hi] = jnp.exp2((s - top) * scale).astype(bf16)

    def mix(u):
        p, h = units[u]
        lo, hi = halves[p]
        o = jnp.dot(pv[u % SLOTS, :hi - lo, :hi], vv[h, :hi, :], preferred_element_type=f32)
        o = (o[:, :HEAD_DIM] / o[:, HEAD_DIM:]).astype(bf16)
        xg[lo:hi, h * HEAD_DIM:(h + 1) * HEAD_DIM] = o
        att[lo:hi, h * HEAD_DIM:(h + 1) * HEAD_DIM] = o

    def send(p, c):
        if p == 0 and c == 0:
            with scope("barwait"):
                pl.semaphore_wait(barrier, chips)
        for b in range(len(bands)):
            if bands[b][0] == halves[p][0]:
                for d in range(1, chips):
                    cross_copy(b, c, d).start()
        side_copy(p, c).start()

    own_starts = [(e, k, j) for e in range(experts) for k, j in quarters]
    far_starts = [(e, d, c, k, j) for c in range(chunks) for d in range(1, chips)
                  for e in range(experts) for k, j in quarters]
    started = [0]

    def start_own(n):
        for at in own_starts[started[0]:started[0] + n]:
            own_weight(*at).start()
        started[0] += n

    def arrive_inputs(u):
        p, h = units[u]
        if h % 2 == 0:
            with scope("inwait"):
                for copy in in_copies(p, h // 2):
                    copy.wait()

    with scope("attend"):
        count = len(units)
        for u in range(2):
            arrive_inputs(u)
            score(u)
        for u in range(2):
            soften(u)
        for u in range(2):
            mix(u)
        send(0, 0)
        for t in range(2, count + 2):
            if t < count:
                if units[t] == (1, 0):
                    set_bias(1)
                arrive_inputs(t)
                score(t)
            if 2 < t < count + 1:
                soften(t - 1)
            if 3 < t:
                mix(t - 2)
                p, h = units[t - 2]
                if h % 2 == 1:
                    send(p, h // 2)
                start_own(-(-len(own_starts) // (count - 2)))
        start_own(len(own_starts))
        for b in range(len(bands)):
            if bands[b][0] not in [lo for lo, _ in halves]:
                for c in range(chunks):
                    for d in range(1, chips):
                        cross_copy(b, c, d).start()

    with scope("startfar"):
        for at in far_starts:
            far_weight(*at).start()

    arrivals = [(b, c, d) for b in range(len(bands)) for c in range(chunks)
                for d in range(1, chips)]
    sent = [0]

    def forward(b, c, d):
        upto = arrivals.index((b, c, d)) + 1
        while sent[0] < upto:
            with scope("fwdwait"):
                cross_copy(*arrivals[sent[0]]).wait_recv()
            pass_copy(*arrivals[sent[0]]).start()
            sent[0] += 1

    def forward_more(n):
        if n > 0:
            forward(*arrivals[min(sent[0] + n, len(arrivals)) - 1])

    def set_gates(e):
        chosen = ids[...] == me * experts + e
        line = jnp.sum(jnp.where(chosen, gates[...], 0.0), axis=0, keepdims=True)
        for r in range(0, rows, 128):
            gsc[e, r:r + 128, :] = jnp.broadcast_to(line[:, r:r + 128], (128, 128)).T

    for i in range(1, 4):
        small_copy(i).wait()
    for e in range(experts):
        with scope("wownwait"):
            for k, j in quarters:
                own_weight(e, k, j).wait()
        with scope("near"):
            set_gates(e)
            if e == 0:
                acc[e] = jnp.dot(xg[:, :width], wv[e, :width, :], preferred_element_type=f32)
                with scope("sidewait"):
                    for p in range(2):
                        for c in range(chunks):
                            side_copy(p, c).wait_recv()
                acc[e] += jnp.dot(xg[:, width:chip_width], wv[e, width:chip_width, :],
                                  preferred_element_type=f32)
            else:
                acc[e] = jnp.dot(xg[:, :chip_width], wv[e, :chip_width, :],
                                 preferred_element_type=f32)
        if e < experts - 1:
            forward_more(min(1, chunks * (chips - 1) - sent[0]))

    with scope("misc"):
        partner = lax.rem(row + dp_size // 2, dp_size)
        own_total, own_moved = row_pairs(lens, row, plan[1, row], docs, rows)
        _, their_moved = row_pairs(lens, partner, plan[1, partner], docs, rows)
        work = own_total - jnp.where(plan[0, row] != row, own_moved, 0)
        work = work + jnp.where(plan[0, partner] != partner, their_moved, 0)
        load[...] = jnp.full((1,), work.astype(f32) * (1.0 / (QBLOCK * QBLOCK)))

    def arrive(b, c, d):
        forward(b, c, d)
        with scope("passwait"):
            pass_copy(b, c, d).wait_recv()
        far_ready(b, c, d)

    def far_ready(b, c, d):
        if b == 0:
            for e in range(experts):
                for k, j in quarters:
                    far_weight(e, d, c, k, j).wait()

    def add_far(b, span):
        lo, hi = bands[b]
        for e in range(experts):
            acc[e, lo:hi, :] += jnp.dot(xg[lo:hi, span], wv[e, span, :],
                                        preferred_element_type=f32)

    rt = 32
    tile = max(owned, 128)

    def close(b, span):
        lo, hi = bands[b]
        for j in list(range(1, chips)) + [0]:
            for at in range(j * columns, (j + 1) * columns, tile):
                cols = slice(at, at + tile)
                for e in range(experts):
                    acc[e, lo:hi, cols] += jnp.dot(xg[lo:hi, span], wv[e, span, cols],
                                                   preferred_element_type=f32)
                for r in range(lo, hi, rt):
                    total = jnp.zeros((rt, tile), f32)
                    for e in range(experts):
                        h = acc[e, r:r + rt, cols] * 0.5
                        total = total + (h * jnp.tanh(h) + h) * jnp.concatenate(
                            [gsc[e, r:r + rt, :]] * (tile // 128), axis=1)
                    total = total.astype(bf16)
                    for i in range(tile // owned):
                        part[at // owned + i, r:r + rt, :] = total[:, i * owned:(i + 1) * owned]
            pair_copy(b, j).start()

    def exchange(b):
        lo, hi = bands[b]
        for d in range(1, chips):
            with scope("pairwait"):
                pair_copy(b, d).wait_recv()
            txx[d - 1, lo:hi, :] = (part[d * 2 + core, lo:hi, :].astype(f32)
                                    + rxd[d, lo:hi, :].astype(f32)).astype(bf16)
            sum_copy(b, d).start()

    def finish(b):
        lo, hi = bands[b]
        with scope("pairwait"):
            pair_copy(b, 0).wait_recv()
        total = part[core, lo:hi, :].astype(f32) + rxd[0, lo:hi, :].astype(f32)
        for d in range(1, chips):
            with scope("sumwait"):
                sum_copy(b, d).wait_recv()
            total = total + rxx[d - 1, lo:hi, :].astype(f32)
        comb[lo:hi, :] = total.astype(bf16)

    steps = [(c, d) for c in range(chunks) for d in range(1, chips)]
    for b in range(len(bands)):
        for i, (c, d) in enumerate(steps[:-1]):
            forward(b, *steps[i + 1])
            arrive(b, c, d)
            with scope(f"far{b}"):
                add_far(b, slice(place(d, c, 0), place(d, c, 0) + step))
            if b > 0 and i == len(steps) // 2:
                exchange(b - 1)
        if b > 0 and len(steps) == 1:
            exchange(b - 1)
        c, d = steps[-1]
        forward(b, c, d)
        if b < last:
            forward(b + 1, *steps[0])
        far_ready(b, c, d)
        with scope(f"half{b}"):
            add_far(b, slice(place(d, c, 0), place(d, c, 0) + ck))
        with scope("passwait"):
            pass_copy(b, c, d).wait_recv()
        with scope(f"close{b}"):
            close(b, slice(place(d, c, 1), place(d, c, 1) + ck))
    exchange(last)
    with scope("finish"):
        for b in range(len(bands)):
            finish(b)

    with scope("endside"):
        for p in range(2):
            for c in range(chunks):
                side_copy(p, c).wait_send()
    with scope("endcross"):
        for b, c, d in arrivals:
            cross_copy(b, c, d).wait_send()
    with scope("endpass"):
        for b, c, d in arrivals:
            pass_copy(b, c, d).wait_send()
    with scope("endsum"):
        for b in range(len(bands)):
            for d in range(chips):
                pair_copy(b, d).wait_send()
            for d in range(1, chips):
                sum_copy(b, d).wait_send()


def emit(att, comb, load, att_hbm, comb_hbm, load_hbm, sem):
    copies = [pltpu.make_async_copy(src, dst, sem.at[i]) for i, (src, dst) in enumerate(
        ((att, att_hbm), (comb, comb_hbm), (load, load_hbm)))]
    for copy in copies:
        copy.start()
    for copy in copies:
        copy.wait()


def shards(dp_size, group, queries, key_states, value_states, doc_lengths, move_plan,
           expert_ids, gate_weights, expert_weight):
    rows, width = queries.shape
    experts, depth, ff = expert_weight.shape
    topk = expert_ids.shape[1]
    chips = group // 2
    chunks = width // (2 * HEAD_DIM)
    heads = width // HEAD_DIM
    owned = ff // group
    half = rows // 2
    nb = len(bands_of(rows))
    bf16, f32, i32 = jnp.bfloat16, jnp.float32, jnp.int32
    hbm = pl.BlockSpec(memory_space=pl.ANY)
    vmem = pl.BlockSpec(memory_space=pltpu.VMEM)
    dma = pltpu.SemaphoreType.DMA
    local = [
        dma((4,)),
        dma((2, chunks, 4)),
        dma((experts, 2, chips)),
        dma((experts, chips - 1, chunks, 2, chips)),
        dma((chips - 1, nb, chunks)),
        dma((2, chunks)),
        dma((chips - 1, nb, chunks)),
        dma((nb, chips)),
        dma((nb, chips - 1)),
    ]

    def scoped(*refs):
        pl.run_scoped(functools.partial(kernel, dp_size, group, *refs), *local)

    outs = pl.pallas_call(
        scoped,
        out_shape=(
            pltpu.VMEM((rows, width), bf16),
            pltpu.VMEM((rows, owned), bf16),
            pltpu.VMEM((1,), f32),
        ),
        in_specs=[hbm] * 8,
        out_specs=(vmem, vmem, vmem),
        scratch_shapes=[
            pltpu.SMEM(doc_lengths.shape, i32),
            pltpu.SMEM(move_plan.shape[::-1], i32),
            pltpu.VMEM((topk, rows), i32),
            pltpu.VMEM((topk, rows), f32),
            pltpu.VMEM((rows, width), bf16),
            pltpu.VMEM((rows, width), bf16),
            pltpu.VMEM((heads, rows, 2 * HEAD_DIM), bf16),
            pltpu.VMEM((SLOTS, half, rows), f32),
            pltpu.VMEM((SLOTS, half, rows), bf16),
            pltpu.VMEM((experts, depth, ff), bf16),
            pltpu.VMEM((rows, depth), bf16),
            pltpu.VMEM((experts, rows, ff), f32),
            pltpu.VMEM((rows, rows), f32),
            pltpu.VMEM((experts, rows, 128), f32),
            pltpu.VMEM((group, rows, owned), bf16),
            pltpu.VMEM((chips, rows, owned), bf16),
            pltpu.VMEM((chips - 1, rows, owned), bf16),
            pltpu.VMEM((chips - 1, rows, owned), bf16),
            dma((chips - 1, nb, chunks)),
            dma((2, chunks)),
            dma((chips - 1, nb, chunks)),
            dma((nb, chips)),
            dma((nb, chips - 1)),
        ],
        compiler_params=pltpu.CompilerParams(
            collective_id=0, has_side_effects=True, vmem_limit_bytes=64_000_000),
    )(queries, key_states, value_states, doc_lengths, move_plan.T, expert_ids.T,
      gate_weights.T, expert_weight)
    return pl.pallas_call(
        emit,
        out_shape=(
            jax.ShapeDtypeStruct((rows, width), bf16),
            jax.ShapeDtypeStruct((rows, owned), bf16),
            jax.ShapeDtypeStruct((1,), f32),
        ),
        in_specs=[vmem, vmem, vmem],
        out_specs=(hbm, hbm, hbm),
        scratch_shapes=[dma((3,))],
    )(*[pltpu.with_memory_space_constraint(out, pltpu.VMEM) for out in outs])


def solution(mesh):
    in_specs = (
        P("dp", "expert"),
        P("dp", "expert"),
        P("dp", "expert"),
        P(),
        P(),
        P("dp", None),
        P("dp", None),
        P("expert", None, None),
    )
    out_specs = (P("dp", "expert"), P("dp", "expert"), P("dp"))
    body = functools.partial(shards, mesh.shape["dp"], mesh.shape["expert"])
    return jax.shard_map(body, mesh=mesh, in_specs=in_specs, out_specs=out_specs, check_vma=False)
```

time: 48.3 us -> 39.3 us (0.81)
  local copies, waits for them, and re-layouts: 3.93 us -> 0 us
  Pallas kernels: 41.7 us -> 38.4 us
  between operations: 2.4 us -> 0.8 us
    unnamed x2 -> x0, local copies, waits for them, and re-layouts: 3.93 us -> none
    pallas_call x1 -> x2, Pallas kernels: 41.7 us -> 38.4 us  [the longest x1 36.7 us: shards(): pl.pallas_call(scoped, out_shape=(pltpu.VMEM((rows, width), bf16), pltpu....]
where the time goes in v1:
time: 39.3 us; the launch traced here: 39.2 us
  Pallas kernels  38.4 us (98%)
  between operations  0.8 us (2%)
    pallas_call x1, Pallas kernels, shards(): pl.pallas_call(scoped, out_shape=(pltpu.VMEM((rows, width), bf16), pltpu....  36.7 us
    pallas_call x1, Pallas kernels, shards(): pl.pallas_call(emit, out_shape=(jax.ShapeDtypeStruct((rows, width), bf16)...  1.63 us

profile of v1, /device:TPU:0, one launch (start us, length us, event | category | flops | bytes accessed | tf_op | source)
XLA Modules:
  0.0 39.2 jit_solution(2974778212700898012)
XLA Ops:
  0.6 36.7 %shard_map.103 = (bf16[512,1024]{1,0:T(8,128)(2,1)S(1)}, bf16[512,256]{1,0:T(8,128)(2,1)S(1)}, f32[1]{0:T(128)}) custom-call(bf16[512,1024]{1,0:T(8,128)(2,1)} %refs_0_.1, bf16[512,1024]{1,0:T(8,128)(2,1)} %refs_1_.1, bf16[512,1024]{1,0:T(8,128)(2,1)} %refs_2_.1, s32[8,8]{1,0:T(8,128)} %refs_3_.1, s32[2,8]{1,0:T(2,128)} %bitcast.5, s32[8,512]{1,0:T(8,128)} %bitcast.3, ...), custom_call_target="tpu_custom_call" | custom-call | tf_op jit(solution)/shard_map/pallas_call | solution.py:484
  37.4 1.6 %shard_map.104 = (bf16[512,1024]{1,0:T(8,128)(2,1)}, bf16[512,256]{1,0:T(8,128)(2,1)}, f32[1]{0:T(128)}) custom-call(bf16[512,1024]{1,0:T(8,128)(2,1)S(1)} %get-tuple-element.6.att, bf16[512,256]{1,0:T(8,128)(2,1)S(1)} %get-tuple-element.7.comb, f32[1]{0:T(128)} %get-tuple-element.8.load), custom_call_target="tpu_custom_call" | custom-call | tf_op jit(solution)/shard_map/pallas_call | solution.py:522
